TPU v7x, 32 devices: a whole 2x2x4 slice. The times are simulated.
32 devices in a mesh: dp: 8 (over y, x, core), expert: 4 (over z).
Axes of the slice: x: 2, y: 2, z: 4, core: 2. Of those that a mesh axis runs over, the one named last changes fastest.
Arguments:
- grad_out: bfloat16 [20480, 1024], P(('dp', 'expert')), may hold values from -3 to 3
- hidden_acts: bfloat16 [20480, 384], P(('dp', 'expert')), may hold values from -0.23925781 to 0.23925781
- expert_ids: int32 [20480], P(('dp', 'expert')), may hold values from 0 to 3, as said below
- down_weight: bfloat16 [4, 384, 1024], P('expert'), may hold values from -0.1875 to 0.1875
- error_in: bfloat16 [8, 4, 384, 1024], P('dp', 'expert'), may hold values from -0.8984375 to 0.8984375
- q_prev: float32 [4, 1024, 32], P('expert'), may hold values from -6 to 6
Outputs:
- grad_hidden: bfloat16 [20480, 384], P(('dp', 'expert'))
- left_factor: float32 [4, 384, 32], P('expert')
- right_factor: float32 [4, 1024, 32], P('expert')
- error_out: bfloat16 [8, 4, 384, 1024], P('dp', 'expert')
Inputs may be any that keep to these rules, and one draw needn't show every extreme that they name: `expert_ids`: the rows of one device name each expert at most 320 times; in every replica some expert is named exactly 320 times by the rows of every device of that replica.
All inputs are finite; a program needn't handle non-finite values.
Results may differ from a plain program's by a relative error of at most 0.0004.
Values may be sent and summed in bfloat16 or wider, within the bound.
No kernel may reach another device: no remote copies, remote signals or barrier semaphores. Data moves between devices by JAX's collectives and lax.ppermute only.
A program may use at most 64 MiB of HBM per device.

v0:
```python
import jax
import jax.numpy as jnp
from jax import lax
from jax.sharding import PartitionSpec as P


def place_rows(expert_list, count):
    onehot = (expert_list[:, None] == jnp.arange(count, dtype=jnp.int32)[None, :]).astype(jnp.int32)
    ranks = jnp.cumsum(onehot, axis=0) - 1
    return jnp.sum(ranks * onehot, axis=1)


def orthonormal(block, gram):
    chol = jnp.linalg.cholesky(gram)
    return lax.linalg.triangular_solve(chol, block, left_side=False, lower=True, transpose_a=True)


def shards(grad_out, hidden_acts, expert_ids, down_weight, error_in, q_prev):
    experts = lax.axis_size("expert")
    row_count = grad_out.shape[0]
    capacity = 2 * row_count // experts
    width = grad_out.shape[1]
    hidden_width = hidden_acts.shape[1]
    position = place_rows(expert_ids, experts)
    slot_index = expert_ids * capacity + position
    grad_buffer = jnp.zeros((experts * capacity, width), jnp.bfloat16).at[slot_index].set(grad_out)
    grad_buffer = grad_buffer.reshape(experts, capacity, width)
    hidden_buffer = (
        jnp.zeros((experts * capacity, hidden_width), jnp.bfloat16).at[slot_index].set(hidden_acts)
    )
    hidden_buffer = hidden_buffer.reshape(experts, capacity, hidden_width)
    weight = down_weight[0]
    grad_recv, hidden_recv = (
        lax.all_to_all(grad_buffer, "expert", split_axis=0, concat_axis=0, tiled=True),
        lax.all_to_all(hidden_buffer, "expert", split_axis=0, concat_axis=0, tiled=True),
    )
    product = lax.dot_general(
        grad_recv, weight, (((2,), (1,)), ((), ())), preferred_element_type=jnp.float32
    )
    back = lax.all_to_all(
        product.astype(jnp.bfloat16), "expert", split_axis=0, concat_axis=0, tiled=True
    )
    grads = lax.dot_general(
        hidden_recv.reshape(-1, hidden_width),
        grad_recv.reshape(-1, width),
        (((0,), (0,)), ((), ())),
        preferred_element_type=jnp.float32,
    )
    grad_hidden = back.reshape(experts * capacity, hidden_width)[slot_index]
    merged = grads + error_in[0, 0].astype(jnp.float32)
    highest = lax.Precision.HIGHEST
    left_local = jnp.dot(merged, q_prev[0], precision=highest)
    left_sum = lax.psum(left_local, "dp")
    gram = jnp.dot(left_sum.T, left_sum, precision=highest)
    left_factor = orthonormal(left_sum, gram)
    right_local = lax.dot_general(merged, left_factor, (((0,), (0,)), ((), ())), precision=highest)
    right_factor = lax.psum(right_local, "dp") / lax.axis_size("dp")
    approx = jnp.dot(left_factor, right_factor.T, precision=highest)
    error_out = (merged - approx).astype(jnp.bfloat16)
    return (grad_hidden, left_factor[None], right_factor[None], error_out[None, None])


def solution(mesh):
    placed = (
        P(("dp", "expert"), None),
        P(("dp", "expert"), None),
        P(("dp", "expert")),
        P("expert", None, None),
        P("dp", "expert", None, None),
        P("expert", None, None),
    )
    return jax.shard_map(
        shards,
        mesh=mesh,
        in_specs=placed,
        out_specs=(
            P(("dp", "expert"), None),
            P("expert", None, None),
            P("expert", None, None),
            P("dp", "expert", None, None),
        ),
        check_vma=False,
    )
```

profile of v0, /device:TPU:0, one launch (start us, length us, event | category | flops | bytes accessed | tf_op | source)
XLA Modules:
  0.0 222.1 jit_solution(1954944167356880882)
XLA Ops:
  7.2 0.0 copy-start
  7.2 0.8 fusion.14
  7.9 1.1 reduce-window.6
  9.1 0.2 slice_reduce_fusion
  9.3 0.2 reduce-window.9
  9.5 0.1 add_bitcast_fusion
  9.5 0.7 fusion.16
  10.3 0.7 compare_select_fusion
  11.0 7.1 %scatter_custom_fusion.1 = bf16[1280,384]{1,0:T(8,128)(2,1)} fusion(s32[640]{0:T(1024)S(1)} %compare_select_fusion, bf16[640,384]{1,0:T(8,128)(2,1)} %param.7, bf16[]{:T(256)} %constant.51.clone.1), kind=kCustom, calls=%fused_computation.10 | custom fusion | bytes 983552 | tf_op jit(solution)/shard_map/scatter | solution.py:29
  18.1 6.3 %all-to-all-start.2 = ((bf16[4,320,384]{2,1,0:T(8,128)(2,1)}), bf16[4,320,384]{2,1,0:T(8,128)(2,1)S(1)}, u32[]{:S(2)}, u32[]{:S(2)}) async-start(bf16[4,320,384]{2,1,0:T(8,128)(2,1)} %bitcast.6), calls=%async_computation.2 | async-start | bytes 1966080 | tf_op jit(solution)/shard_map/all_to_all | solution.py:35
  24.4 8.2 %scatter_custom_fusion = bf16[1280,1024]{1,0:T(8,128)(2,1)} fusion(s32[640]{0:T(1024)S(1)} %compare_select_fusion, bf16[640,1024]{1,0:T(8,128)(2,1)} %param.6, bf16[]{:T(256)} %constant.51.clone.1), kind=kCustom, calls=%fused_computation.6 | custom fusion | bytes 2621952 | tf_op jit(solution)/shard_map/scatter | solution.py:26
  32.6 16.1 %all-to-all-done.2 = bf16[4,320,384]{2,1,0:T(8,128)(2,1)S(1)} async-done(((bf16[4,320,384]{2,1,0:T(8,128)(2,1)}), bf16[4,320,384]{2,1,0:T(8,128)(2,1)S(1)}, u32[]{:S(2)}, u32[]{:S(2)}) %all-to-all-start.2) | async-done | bytes 983072 | tf_op jit(solution)/shard_map/all_to_all | solution.py:35
  48.7 0.0 copy-start.2
  48.7 62.7 %all_to_all.15 = bf16[4,320,1024]{2,1,0:T(8,128)(2,1)S(1)} all-to-all(bf16[4,320,1024]{2,1,0:T(8,128)(2,1)} %bitcast.56), channel_id=1, replica_groups=mesh['dp'=8,'expert'=4] {'expert'}, dimensions={0} | all-to-all | bytes 5242880 | tf_op jit(solution)/shard_map/all_to_all | solution.py:34
  111.5 0.0 copy-done.2
  111.5 0.0 copy-start.1
  111.5 0.0 copy-start.5
  111.5 1.2 convert_add_fusion
  112.7 0.3 copy-done.1
  113.0 0.0 copy-done.5
  113.0 1.5 fusion.6
  114.5 23.2 %psum.14 = f32[384,32]{0,1:T(8,128)S(1)} all-reduce(f32[384,32]{0,1:T(8,128)S(1)} %fusion.6), channel_id=1, replica_groups=mesh['dp'=8,'expert'=4] {'dp'}, use_global_device_ids=true, to_apply=%region_5.6 | all-reduce | flops 12288 | bytes 98304 | tf_op jit(solution)/shard_map/psum | solution.py:53
  137.7 0.2 fusion.18
  137.9 0.1 copy.11
  138.0 0.0 copy-done
  138.0 4.3 %convolution_convert_fusion = bf16[4,320,384]{2,1,0:T(8,128)(2,1)} fusion(bf16[4,320,1024]{2,1,0:T(8,128)(2,1)} %copy-done.1, bf16[1,384,1024]{2,1,0:T(8,128)(2,1)S(1)} %copy-done), kind=kOutput, calls=%fused_computation.5 | convolution fusion | flops 1007124480 | bytes 4390912 | tf_op jit(solution)/shard_map/dot_general | solution.py:37
  142.3 3.6 %all-to-all-start.1 = ((bf16[4,320,384]{2,1,0:T(8,128)(2,1)}), bf16[4,320,384]{2,1,0:T(8,128)(2,1)S(1)}, u32[]{:S(2)}, u32[]{:S(2)}) async-start(bf16[4,320,384]{2,1,0:T(8,128)(2,1)} %convolution_convert_fusion), calls=%async_computation.1 | async-start | bytes 1966080 | tf_op jit(solution)/shard_map/all_to_all | solution.py:40
  145.8 0.2 all-reduce.2.cloned.1.call-start
  146.0 2.9 %cholesky.16 = f32[32,32]{1,0:T(8,128)S(1)} custom-call(f32[32,32]{1,0:T(8,128)S(1)} %fusion.13), custom_call_target="Cholesky" | custom-call | tf_op jit(solution)/shard_map/jit(cholesky)/cholesky | solution.py:14
  149.0 0.6 compare_reduce_fusion
  149.6 0.7 fusion.10
  150.3 2.5 %custom-call.6 = f32[1,32,32]{1,2,0:T(8,128)S(1)} custom-call(f32[1,32,32]{2,1,0:T(8,128)S(1)} %fusion.10), custom_call_target="InvertDiagBlocksLowerTriangular" | custom-call | tf_op jit(solution)/shard_map/triangular_solve | solution.py:15
  152.7 0.2 fusion.11
  153.0 0.0 copy-start.4
  153.0 1.7 fusion.19
  154.7 0.0 all-reduce.2.cloned.1.call-update
  154.7 53.3 %all-reduce.2.cloned.1.call-done = f32[1024,32]{0,1:T(8,128)} async-done(((f32[1024,32]{0,1:T(8,128)}), f32[1024,32]{0,1:T(8,128)}) %all-reduce.2.cloned.1.call-update) | async-done | bytes 131088 | tf_op jit(solution)/shard_map/psum | solution.py:57
  208.1 0.0 copy-start.3
  208.1 3.3 %fusion.2 = bf16[1,1,384,1024]{3,2,1,0:T(8,128)(2,1)} fusion(f32[384,1024]{1,0:T(8,128)S(1)} %convert_add_fusion, f32[384,32]{0,1:T(8,128)S(1)} %fusion.11, f32[1024,32]{0,1:T(8,128)} %all-reduce.2.cloned.1.call-done), kind=kOutput, calls=%fused_computation.8 | convolution fusion | flops 151814144 | bytes 2539520 | tf_op jit(solution)/shard_map/dot_general | solution.py:58
  211.4 0.0 copy-done.4
  211.4 0.0 copy-done.3
  211.4 0.7 multiply_bitcast_fusion
  212.0 0.0 all-to-all-done.1
  212.0 3.2 %gather_fusion = bf16[640,384]{1,0:T(8,128)(2,1)} fusion(bf16[1280,384]{1,0:T(8,128)(2,1)S(1)} %bitcast.55, s32[1024]{0:T(1024)S(1)} %pad_clamp_fusion), kind=kCustom, calls=%fused_computation | custom fusion | bytes 985600 | tf_op jit(solution)/shard_map/gather | solution.py:49
  (3 shorter events, 0.0 us)
Async XLA Ops:
  7.2 130.8 %copy-start = (bf16[1,384,1024]{2,1,0:T(8,128)(2,1)S(1)}, bf16[1,384,1024]{2,1,0:T(8,128)(2,1)}, u32[]{:S(2)}) copy-start(bf16[1,384,1024]{2,1,0:T(8,128)(2,1)} %param.9) | copy-start | bytes 2359300
  18.1 30.7 %all-to-all-start.2 = ((bf16[4,320,384]{2,1,0:T(8,128)(2,1)}), bf16[4,320,384]{2,1,0:T(8,128)(2,1)S(1)}, u32[]{:S(2)}, u32[]{:S(2)}) async-start(bf16[4,320,384]{2,1,0:T(8,128)(2,1)} %bitcast.6), calls=%async_computation.2 | async-start | bytes 1966080 | tf_op jit(solution)/shard_map/all_to_all | solution.py:35
  48.7 62.8 %copy-start.2 = (bf16[1,1,384,1024]{3,2,1,0:T(8,128)(2,1)S(1)}, bf16[1,1,384,1024]{3,2,1,0:T(8,128)(2,1)}, u32[]{:S(2)}) copy-start(bf16[1,1,384,1024]{3,2,1,0:T(8,128)(2,1)} %param.10) | copy-start | bytes 2359300
  111.5 1.5 copy-start.1
  111.5 1.5 copy-start.5
  142.3 69.8 %all-to-all-start.1 = ((bf16[4,320,384]{2,1,0:T(8,128)(2,1)}), bf16[4,320,384]{2,1,0:T(8,128)(2,1)S(1)}, u32[]{:S(2)}, u32[]{:S(2)}) async-start(bf16[4,320,384]{2,1,0:T(8,128)(2,1)} %convolution_convert_fusion), calls=%async_computation.1 | async-start | bytes 1966080 | tf_op jit(solution)/shard_map/all_to_all | solution.py:40
  145.8 62.2 %all-reduce.2.cloned.1.call-start = ((), (), s32[]{:S(2)}) async-start(), calls=%async_computation.3 | async-start | bytes 262144 | tf_op jit(solution)/shard_map/psum | solution.py:57
  153.0 58.4 %copy-start.4 = (f32[384,32]{0,1:T(8,128)}, f32[384,32]{0,1:T(8,128)S(1)}, u32[]{:S(2)}) copy-start(f32[384,32]{0,1:T(8,128)S(1)} %fusion.11) | copy-start | bytes 147460
  208.1 3.3 %copy-start.3 = (f32[1024,32]{0,1:T(8,128)S(1)}, f32[1024,32]{0,1:T(8,128)}, u32[]{:S(2)}) copy-start(f32[1024,32]{0,1:T(8,128)} %all-reduce.2.cloned.1.call-done) | copy-start | bytes 393220
Sparse Core Ops, SparseCore 0:
  154.8 53.1 all-reduce.1
where the time goes:
time: 223 us; the launch traced here: 222 us
  blocking collectives  86 us (39%)
  waiting for transfers between devices  69.4 us (31%)
  local copies, waits for them, and re-layouts  19.1 us (9%)
  between operations  14.1 us (6%)
  matrix products  12.4 us (6%)
  other arithmetic  10.9 us (5%)
  starting transfers between devices  10.1 us (5%)
    all_to_all x1, blocking collectives, shards(): lax.all_to_all(grad_buffer, 'expert', split_axis=0, concat_axis=0, tiled=...  62.7 us
    psum x1, waiting for transfers between devices, shards(): right_factor = lax.psum(right_local, 'dp') / lax.axis_size('dp')  53.3 us
    psum x1, blocking collectives, shards(): left_sum = lax.psum(left_local, 'dp')  23.2 us
    all_to_all x1, waiting for transfers between devices, shards(): lax.all_to_all(hidden_buffer, 'expert', split_axis=0, concat_axis=0, tile...  16.1 us
    scatter x1, local copies, waits for them, and re-layouts, shards(): jnp.zeros((experts * capacity, width), jnp.bfloat16).at[slot_index]  8.24 us
    scatter x1, local copies, waits for them, and re-layouts, shards(): jnp.zeros((experts * capacity, hidden_width), jnp.bfloat16).at[slot_index]  7.1 us
    all_to_all x1, starting transfers between devices, shards(): lax.all_to_all(hidden_buffer, 'expert', split_axis=0, concat_axis=0, tile...  6.35 us
  transfers between devices with their start and end apart: 3, of which 2 were waited for; matrix products, arithmetic and copies ran while one was open for 9% of the time, Pallas kernels for 0%

commit v1 on v0

--- a/solution.py
+++ b/solution.py
@@ -54,7 +54,7 @@
     gram = jnp.dot(left_sum.T, left_sum, precision=highest)
     left_factor = orthonormal(left_sum, gram)
     right_local = lax.dot_general(merged, left_factor, (((0,), (0,)), ((), ())), precision=highest)
-    right_factor = lax.psum(right_local, "dp") / lax.axis_size("dp")
+    right_factor = jnp.sum(lax.all_gather(right_local, "dp"), axis=0) / lax.axis_size("dp")
     approx = jnp.dot(left_factor, right_factor.T, precision=highest)
     error_out = (merged - approx).astype(jnp.bfloat16)
     return (grad_hidden, left_factor[None], right_factor[None], error_out[None, None])

time: 223 us -> 192 us (0.86)
  waiting for transfers between devices: 69.4 us -> 38.2 us
    psum x1 -> x0, waiting for transfers between devices: 53.3 us -> none  [shards(): right_factor = lax.psum(right_local, 'dp') / lax.axis_size('dp')]
    all_to_all x1, waiting for transfers between devices: 0.01 us -> 22.1 us  [shards(): lax.all_to_all(product.astype(jnp.bfloat16), 'expert', split_axis=0, conc...]
  transfers between devices with their start and end apart: 3 -> 3, of which waited for: 2 -> 2; matrix products, arithmetic and copies ran while one was open for 9% -> 8% of each run, Pallas kernels for 0% -> 0%
where the time goes in v1:
time: 192 us
  blocking collectives  86 us (45%)
  waiting for transfers between devices  38.2 us (20%)
  local copies, waits for them, and re-layouts  21 us (11%)
  between operations  14.1 us (7%)
  matrix products  11.4 us (6%)
  other arithmetic  11.2 us (6%)
  starting transfers between devices  9.92 us (5%)
    all_to_all x1, blocking collectives, shards(): lax.all_to_all(grad_buffer, 'expert', split_axis=0, concat_axis=0, tiled=...  62.7 us
    psum x1, blocking collectives, shards(): left_sum = lax.psum(left_local, 'dp')  23.2 us
    all_to_all x1, waiting for transfers between devices, shards(): lax.all_to_all(product.astype(jnp.bfloat16), 'expert', split_axis=0, conc...  22.1 us
    all_to_all x1, waiting for transfers between devices, shards(): lax.all_to_all(hidden_buffer, 'expert', split_axis=0, concat_axis=0, tile...  16.1 us
    scatter x1, local copies, waits for them, and re-layouts, shards(): jnp.zeros((experts * capacity, width), jnp.bfloat16).at[slot_index]  8.24 us
    scatter x1, local copies, waits for them, and re-layouts, shards(): jnp.zeros((experts * capacity, hidden_width), jnp.bfloat16).at[slot_index]  7.1 us
    all_to_all x1, starting transfers between devices, shards(): lax.all_to_all(hidden_buffer, 'expert', split_axis=0, concat_axis=0, tile...  6.35 us
    dot_general x1, matrix products, shards(): lax.dot_general(grad_recv, weight, (((2,), (1,)), ((), ())), preferred_el...  4.22 us
  transfers between devices with their start and end apart: 3, of which 2 were waited for; matrix products, arithmetic and copies ran while one was open for 8% of the time, Pallas kernels for 0%

profile of v1, /device:TPU:0, one launch (start us, length us, event | category | flops | bytes accessed | tf_op | source)
XLA Modules:
  0.0 191.8 jit_solution(1631044556661522230)
XLA Ops:
  7.2 0.0 copy-start
  7.2 0.8 fusion.14
  7.9 1.1 reduce-window.6
  9.1 0.2 slice_reduce_fusion
  9.3 0.2 reduce-window.9
  9.5 0.1 add_bitcast_fusion
  9.5 0.7 fusion.16
  10.3 0.7 compare_select_fusion
  11.0 7.1 %scatter_custom_fusion.1 = bf16[1280,384]{1,0:T(8,128)(2,1)} fusion(s32[640]{0:T(1024)S(1)} %compare_select_fusion, bf16[640,384]{1,0:T(8,128)(2,1)} %param.7, bf16[]{:T(256)} %constant.52.clone.1), kind=kCustom, calls=%fused_computation.11 | custom fusion | bytes 983552 | tf_op jit(solution)/shard_map/scatter | solution.py:29
  18.1 6.3 %all-to-all-start.2 = ((bf16[4,320,384]{2,1,0:T(8,128)(2,1)}), bf16[4,320,384]{2,1,0:T(8,128)(2,1)S(1)}, u32[]{:S(2)}, u32[]{:S(2)}) async-start(bf16[4,320,384]{2,1,0:T(8,128)(2,1)} %bitcast.6), calls=%async_computation.2 | async-start | bytes 1966080 | tf_op jit(solution)/shard_map/all_to_all | solution.py:35
  24.4 0.0 all-gather.3.cloned.1.call-start
  24.4 8.2 %scatter_custom_fusion = bf16[1280,1024]{1,0:T(8,128)(2,1)} fusion(s32[640]{0:T(1024)S(1)} %compare_select_fusion, bf16[640,1024]{1,0:T(8,128)(2,1)} %param.6, bf16[]{:T(256)} %constant.52.clone.1), kind=kCustom, calls=%fused_computation.6 | custom fusion | bytes 2621952 | tf_op jit(solution)/shard_map/scatter | solution.py:26
  32.6 16.1 %all-to-all-done.2 = bf16[4,320,384]{2,1,0:T(8,128)(2,1)S(1)} async-done(((bf16[4,320,384]{2,1,0:T(8,128)(2,1)}), bf16[4,320,384]{2,1,0:T(8,128)(2,1)S(1)}, u32[]{:S(2)}, u32[]{:S(2)}) %all-to-all-start.2) | async-done | bytes 983072 | tf_op jit(solution)/shard_map/all_to_all | solution.py:35
  48.7 0.0 copy-start.2
  48.7 62.7 %all_to_all.15 = bf16[4,320,1024]{2,1,0:T(8,128)(2,1)S(1)} all-to-all(bf16[4,320,1024]{2,1,0:T(8,128)(2,1)} %bitcast.61), channel_id=1, replica_groups=mesh['dp'=8,'expert'=4] {'expert'}, dimensions={0} | all-to-all | bytes 5242880 | tf_op jit(solution)/shard_map/all_to_all | solution.py:34
  111.5 0.0 copy-done.2
  111.5 0.0 copy-start.1
  111.5 0.0 copy-start.4
  111.5 1.2 convert_add_fusion
  112.7 0.3 copy-done.1
  113.0 0.0 copy-done.4
  113.0 1.5 fusion.6
  114.5 23.2 %psum.7 = f32[384,32]{0,1:T(8,128)S(1)} all-reduce(f32[384,32]{0,1:T(8,128)S(1)} %fusion.6), channel_id=1, replica_groups=mesh['dp'=8,'expert'=4] {'dp'}, use_global_device_ids=true, to_apply=%region_5.6 | all-reduce | flops 12288 | bytes 98304 | tf_op jit(solution)/shard_map/psum | solution.py:53
  137.7 0.2 fusion.18
  137.9 0.1 copy.11
  138.0 2.9 %cholesky.16 = f32[32,32]{1,0:T(8,128)S(1)} custom-call(f32[32,32]{1,0:T(8,128)S(1)} %fusion.13), custom_call_target="Cholesky" | custom-call | tf_op jit(solution)/shard_map/jit(cholesky)/cholesky | solution.py:14
  141.0 0.6 compare_reduce_fusion
  141.6 0.7 fusion.10
  142.3 2.4 %custom-call.6 = f32[1,32,32]{1,2,0:T(8,128)S(1)} custom-call(f32[1,32,32]{2,1,0:T(8,128)S(1)} %fusion.10), custom_call_target="InvertDiagBlocksLowerTriangular" | custom-call | tf_op jit(solution)/shard_map/triangular_solve | solution.py:15
  144.7 0.3 fusion.11
  145.0 0.0 copy-start.3
  145.0 1.7 fusion.19
  146.7 0.0 all-gather.3.cloned.1.call-update
  146.7 0.0 copy-done
  146.7 4.2 %convolution_convert_fusion = bf16[4,320,384]{2,1,0:T(8,128)(2,1)} fusion(bf16[4,320,1024]{2,1,0:T(8,128)(2,1)} %copy-done.1, bf16[1,384,1024]{2,1,0:T(8,128)(2,1)S(1)} %copy-done), kind=kOutput, calls=%fused_computation.5 | convolution fusion | flops 1007124480 | bytes 4390912 | tf_op jit(solution)/shard_map/dot_general | solution.py:37
  150.9 3.6 %all-to-all-start.1 = ((bf16[4,320,384]{2,1,0:T(8,128)(2,1)}), bf16[4,320,384]{2,1,0:T(8,128)(2,1)S(1)}, u32[]{:S(2)}, u32[]{:S(2)}) async-start(bf16[4,320,384]{2,1,0:T(8,128)(2,1)} %convolution_convert_fusion), calls=%async_computation.1 | async-start | bytes 1966080 | tf_op jit(solution)/shard_map/all_to_all | solution.py:40
  154.5 22.1 %all-to-all-done.1 = bf16[4,320,384]{2,1,0:T(8,128)(2,1)S(1)} async-done(((bf16[4,320,384]{2,1,0:T(8,128)(2,1)}), bf16[4,320,384]{2,1,0:T(8,128)(2,1)S(1)}, u32[]{:S(2)}, u32[]{:S(2)}) %all-to-all-start.1) | async-done | bytes 983072 | tf_op jit(solution)/shard_map/all_to_all | solution.py:40
  176.6 3.2 %gather_fusion = bf16[640,384]{1,0:T(8,128)(2,1)} fusion(bf16[1280,384]{1,0:T(8,128)(2,1)S(1)} %bitcast.60, s32[1024]{0:T(1024)S(1)} %pad_clamp_fusion), kind=kCustom, calls=%fused_computation | custom fusion | bytes 985600 | tf_op jit(solution)/shard_map/gather | solution.py:49
  179.8 0.0 all-gather.3.cloned.1.call-done
  179.8 1.8 copy.13
  181.7 0.3 bitcast_reduce_fusion
  181.9 0.7 multiply_bitcast_fusion
  182.6 0.0 copy-done.3
  182.6 2.3 %fusion.2 = bf16[1,1,384,1024]{3,2,1,0:T(8,128)(2,1)} fusion(f32[384,1024]{1,0:T(8,128)S(1)} %convert_add_fusion, f32[384,32]{0,1:T(8,128)S(1)} %fusion.11, f32[1024,32]{0,1:T(8,128)S(1)} %bitcast_reduce_fusion), kind=kOutput, calls=%fused_computation.8 | convolution fusion | flops 151814144 | bytes 2539520 | tf_op jit(solution)/shard_map/dot_general | solution.py:58
  (3 shorter events, 0.0 us)
Async XLA Ops:
  7.2 139.5 %copy-start = (bf16[1,384,1024]{2,1,0:T(8,128)(2,1)S(1)}, bf16[1,384,1024]{2,1,0:T(8,128)(2,1)}, u32[]{:S(2)}) copy-start(bf16[1,384,1024]{2,1,0:T(8,128)(2,1)} %param.9) | copy-start | bytes 2359300
  18.1 30.7 %all-to-all-start.2 = ((bf16[4,320,384]{2,1,0:T(8,128)(2,1)}), bf16[4,320,384]{2,1,0:T(8,128)(2,1)S(1)}, u32[]{:S(2)}, u32[]{:S(2)}) async-start(bf16[4,320,384]{2,1,0:T(8,128)(2,1)} %bitcast.6), calls=%async_computation.2 | async-start | bytes 1966080 | tf_op jit(solution)/shard_map/all_to_all | solution.py:35
  24.4 155.4 %all-gather.3.cloned.1.call-start = ((), (), s32[]{:S(2)}) async-start(), calls=%async_computation.3 | async-start | bytes 1179648 | tf_op jit(solution)/shard_map/all_gather | solution.py:57
  48.7 62.8 %copy-start.2 = (bf16[1,1,384,1024]{3,2,1,0:T(8,128)(2,1)S(1)}, bf16[1,1,384,1024]{3,2,1,0:T(8,128)(2,1)}, u32[]{:S(2)}) copy-start(bf16[1,1,384,1024]{3,2,1,0:T(8,128)(2,1)} %param.10) | copy-start | bytes 2359300
  111.5 1.5 copy-start.1
  111.5 1.5 copy-start.4
  145.0 37.6 %copy-start.3 = (f32[384,32]{0,1:T(8,128)}, f32[384,32]{0,1:T(8,128)S(1)}, u32[]{:S(2)}) copy-start(f32[384,32]{0,1:T(8,128)S(1)} %fusion.11) | copy-start | bytes 147460
  150.9 25.7 %all-to-all-start.1 = ((bf16[4,320,384]{2,1,0:T(8,128)(2,1)}), bf16[4,320,384]{2,1,0:T(8,128)(2,1)S(1)}, u32[]{:S(2)}, u32[]{:S(2)}) async-start(bf16[4,320,384]{2,1,0:T(8,128)(2,1)} %convolution_convert_fusion), calls=%async_computation.1 | async-start | bytes 1966080 | tf_op jit(solution)/shard_map/all_to_all | solution.py:40
Sparse Core Ops, SparseCore 0:
  146.8 21.4 all-gather.2
